TPU v7x, 512 devices: a whole 4x8x8 slice. The times are simulated.
512 devices in a mesh: row: 32 (over y_lo, x, core), col: 8 (over z), dp: 2 (over y_hi).
Axes of the slice: x: 4, y: 8 (y_hi: 2, y_lo: 4; y = y_hi * 4 + y_lo), z: 8, core: 2. Of those that a mesh axis runs over, the one named last changes fastest.
Arguments:
- pixels: bfloat16 [2, 3, 1024, 1024], P('dp', None, 'row', 'col'), may hold values from -6 to 6
- cotangent: bfloat16 [2, 256, 256, 1024], P('dp', 'row', 'col'), may hold values from -6 to 6
- embed_weight: bfloat16 [48, 1024], replicated, may hold values from -0.875 to 0.875
- embed_bias: float32 [1024], replicated, may hold values from -4 to 4
- layer_norm_gain: float32 [1024], replicated, may hold values from 0.5 to 1.5
- qkv_weight: bfloat16 [1024, 2304], P('row', ('col', 'dp')), may hold values from -0.1875 to 0.1875
- out_weight: bfloat16 [768, 1024], P('row', ('col', 'dp')), may hold values from -0.21875 to 0.21875
- bias_table: float32 [12, 225], replicated, may hold values from -4 to 404
- rel_index: int32 [64, 64], replicated, may hold values from 0 to 224
- shifts: int32 [2, 2], P('dp'), may hold values from 1 to 7
Outputs:
- out_weight_grad: float32 [768, 1024], P('row', ('col', 'dp'))
- embed_weight_grad: float32 [48, 1024], replicated
- embed_bias_grad: float32 [1024], replicated
- norm_gain_grad: float32 [1024], replicated
- bias_table_grad: float32 [12, 225], replicated
Inputs may be any that keep to these rules, and one draw needn't show every extreme that they name: `rel_index`: each entry names one of the 225 columns of bias_table.
All inputs are finite; a program needn't handle non-finite values.
Results may differ from a plain program's by a relative error of at most 0.023.
Values may be sent and summed in bfloat16 or wider, within the bound.
No kernel may reach another device: no remote copies, remote signals or barrier semaphores. Data moves between devices by JAX's collectives and lax.ppermute only.
A program may use at most 64 MiB of HBM per device.

v0:
```python
import jax
import jax.numpy as jnp
from jax import lax
from jax.sharding import PartitionSpec as P

WIN = 8
PATCH = 4
norm_epsilon = 1e-05


def laid_out(blocks, dim):
    blocks = jnp.moveaxis(blocks, 0, dim)
    lengths = blocks.shape
    return blocks.reshape(*lengths[:dim], lengths[dim] * lengths[dim + 1], *lengths[dim + 2 :])


def exchange(blocks, axis):
    return lax.all_to_all(blocks, axis, split_axis=0, concat_axis=0, tiled=True)


def spread(line, axis):
    copies = jnp.broadcast_to(line[None], (lax.axis_size(axis), *line.shape))
    return exchange(copies, axis)


def gather_together(arrays, axis, dims):
    line = jnp.concatenate([a.reshape(-1) for a in arrays])
    lines, at, gathered = (spread(line, axis), 0, [])
    for a, dim in zip(arrays, dims):
        blocks = lines[:, at : at + a.size].reshape(-1, *a.shape)
        gathered.append(laid_out(blocks, dim))
        at += a.size
    return tuple(gathered)


def from_behind(value, axis, steps):
    count = lax.axis_size(axis)
    pairs = [(source, (source + steps) % count) for source in range(count)]
    return lax.ppermute(value, axis, pairs)


def in_blocks(x, dim, length):
    before, after = (x.shape[:dim], x.shape[dim + 1 :])
    return jnp.moveaxis(x.reshape(*before, length, -1, *after), dim, 0)


def summed_on_arrival(x, axis, dim):
    blocks = in_blocks(x, dim, lax.axis_size(axis))
    arrived = lax.all_to_all(blocks, axis, split_axis=0, concat_axis=0, tiled=True)
    return arrived.astype(jnp.float32).sum(axis=0)


def make_patches(pixel_block):
    images, channels, pixel_rows, pixel_cols = pixel_block.shape
    grid_rows = pixel_rows // PATCH
    grid_cols = pixel_cols // PATCH
    shaped = pixel_block.reshape(images, channels, grid_rows, PATCH, grid_cols, PATCH)
    return shaped.transpose(0, 2, 4, 1, 3, 5).reshape(
        images, grid_rows, grid_cols, channels * PATCH * PATCH
    )


def embed_cells(patches, embed_weight, embed_bias):
    return (jnp.dot(patches, embed_weight, preferred_element_type=jnp.float32) + embed_bias).astype(
        jnp.bfloat16
    )


def window_split(block):
    rows_all, cols_all, features = block.shape
    shaped = block.reshape(rows_all // WIN, WIN, cols_all // WIN, WIN, features)
    return shaped.transpose(0, 2, 1, 3, 4).reshape(-1, WIN * WIN, features)


def window_join(windows, rows_all, cols_all):
    features = windows.shape[-1]
    shaped = windows.reshape(rows_all // WIN, cols_all // WIN, WIN, WIN, features)
    return shaped.transpose(0, 2, 1, 3, 4).reshape(rows_all, cols_all, features)


def splice_after(own_block, borrowed, offsets, along_dim):
    length = own_block.shape[along_dim]

    def single(own_item, borrowed_item, offset):
        joined = jnp.concatenate([own_item, borrowed_item], along_dim - 1)
        return lax.dynamic_slice_in_dim(joined, offset, length, along_dim - 1)

    return jax.vmap(single)(own_block, borrowed, offsets)


def attend_forward(cell_windows, labels, layer_norm_gain, qkv_full, bias_full):
    window_count, cell_count, features = cell_windows.shape
    head_count = bias_full.shape[0]
    inner_width = qkv_full.shape[1] // 3
    head_size = inner_width // head_count
    score_scale = head_size ** (-0.5)
    flat_rows = cell_windows.reshape(-1, features).astype(jnp.float32)
    average = jnp.mean(flat_rows, axis=-1, keepdims=True)
    centered_input = flat_rows - average
    inverse_deviation = lax.rsqrt(
        jnp.mean(centered_input * centered_input, axis=-1, keepdims=True) + norm_epsilon
    )
    standardized_rows = centered_input * inverse_deviation
    normalized_rows = (standardized_rows * layer_norm_gain).astype(jnp.bfloat16)
    projected = jnp.dot(normalized_rows, qkv_full, preferred_element_type=jnp.float32).astype(
        jnp.bfloat16
    )
    head_shape = (window_count, cell_count, head_count, head_size)
    query_rows = projected[:, :inner_width].reshape(head_shape)
    key_vectors = projected[:, inner_width : 2 * inner_width].reshape(head_shape)
    value_rows = projected[:, 2 * inner_width :].reshape(head_shape)
    scores = (
        jnp.einsum("wmhd,wnhd->whmn", query_rows, key_vectors, preferred_element_type=jnp.float32)
        * score_scale
        + bias_full[None]
    )
    same_region = labels[:, None, :, None] == labels[:, None, None, :]
    scores = jnp.where(same_region, scores, -1e30)
    row_peak = jnp.max(scores, axis=-1, keepdims=True)
    exp_scores = jnp.exp(scores - row_peak)
    attention_weights = exp_scores / jnp.sum(exp_scores, axis=-1, keepdims=True)
    reduced_probability = attention_weights.astype(jnp.bfloat16)
    attended = jnp.einsum(
        "whmn,wnhd->wmhd", reduced_probability, value_rows, preferred_element_type=jnp.float32
    ).astype(jnp.bfloat16)
    stored_residuals = (
        standardized_rows,
        inverse_deviation,
        query_rows,
        key_vectors,
        value_rows,
        attention_weights,
        reduced_probability,
    )
    return (stored_residuals, attended.reshape(-1, inner_width))


def attend_backward(stored_residuals, d_attended, layer_norm_gain, qkv_full):
    (
        standardized_rows,
        inverse_deviation,
        query_rows,
        key_vectors,
        value_rows,
        attention_weights,
        reduced_probability,
    ) = stored_residuals
    head_shape = query_rows.shape
    score_scale = head_shape[3] ** (-0.5)
    total_row_count = standardized_rows.shape[0]
    inner_width = head_shape[2] * head_shape[3]
    d_heads = d_attended.reshape(head_shape)
    d_prob = jnp.einsum("wmhd,wnhd->whmn", d_heads, value_rows, preferred_element_type=jnp.float32)
    d_values = jnp.einsum(
        "whmn,wmhd->wnhd", reduced_probability, d_heads, preferred_element_type=jnp.float32
    ).astype(jnp.bfloat16)
    d_scores = attention_weights * (
        d_prob - jnp.sum(attention_weights * d_prob, axis=-1, keepdims=True)
    )
    table_part = jnp.sum(d_scores, axis=0)
    d_low = d_scores.astype(jnp.bfloat16)
    d_queries = (
        jnp.einsum("whmn,wnhd->wmhd", d_low, key_vectors, preferred_element_type=jnp.float32)
        * score_scale
    ).astype(jnp.bfloat16)
    d_keys = (
        jnp.einsum("whmn,wmhd->wnhd", d_low, query_rows, preferred_element_type=jnp.float32)
        * score_scale
    ).astype(jnp.bfloat16)
    d_projected = jnp.concatenate(
        [
            d_queries.reshape(total_row_count, inner_width),
            d_keys.reshape(total_row_count, inner_width),
            d_values.reshape(total_row_count, inner_width),
        ],
        axis=1,
    )
    normalized_gradient = lax.dot_general(
        d_projected, qkv_full, (((1,), (1,)), ((), ())), preferred_element_type=jnp.float32
    )
    gain_contribution = jnp.sum(normalized_gradient * standardized_rows, axis=0)
    scaled_rows = normalized_gradient * layer_norm_gain
    branch_gradient = inverse_deviation * (
        scaled_rows
        - jnp.mean(scaled_rows, axis=-1, keepdims=True)
        - standardized_rows * jnp.mean(scaled_rows * standardized_rows, axis=-1, keepdims=True)
    )
    return (branch_gradient.astype(jnp.bfloat16), gain_contribution, table_part)


def on_device(
    pixels,
    cotangent,
    embed_weight,
    embed_bias,
    layer_norm_gain,
    qkv_weight,
    out_weight,
    bias_table,
    rel_index,
    shifts,
):
    images, rows_dev, cols_dev, features = cotangent.shape
    head_count = bias_table.shape[0]
    grid_rows = rows_dev * lax.axis_size("row")
    grid_cols = cols_dev * lax.axis_size("col")
    row_shift = shifts[:, 0]
    col_shift = shifts[:, 1]
    qkv_columns, out_columns = gather_together((qkv_weight, out_weight), ("col", "dp"), (1, 1))
    rows_qkv, width_qkv = qkv_columns.shape
    out_tall = out_columns.reshape(rows_qkv, -1)
    weights = lax.all_gather(
        jnp.concatenate([qkv_columns, out_tall], axis=1), "row", axis=0, tiled=True
    )
    qkv_full = weights[:, :width_qkv]
    out_full = weights[:, width_qkv:].reshape(-1, features)
    patches = make_patches(pixels)
    below = from_behind((pixels, cotangent), "row", -1)
    moved_pixels = splice_after(pixels, below[0], row_shift * PATCH, 2)
    shifted_cot = splice_after(cotangent, below[1], row_shift, 1)
    beside = from_behind((moved_pixels[:, :, :, : WIN * PATCH], shifted_cot[:, :, :WIN]), "col", -1)
    moved_pixels = splice_after(moved_pixels, beside[0], col_shift * PATCH, 3)
    shifted_cot = splice_after(shifted_cot, beside[1], col_shift, 2)
    moved_patches = make_patches(moved_pixels)
    shifted = embed_cells(moved_patches, embed_weight, embed_bias)
    row_ids = lax.axis_index("row") * rows_dev + jnp.arange(rows_dev, dtype=jnp.int32)
    col_ids = lax.axis_index("col") * cols_dev + jnp.arange(cols_dev, dtype=jnp.int32)
    row_part = (row_ids[None, :] >= grid_rows - row_shift[:, None]).astype(jnp.int32)
    col_part = (col_ids[None, :] >= grid_cols - col_shift[:, None]).astype(jnp.int32)
    region = 2 * row_part[:, :, None] + col_part[:, None, :]
    labels = window_split(region.reshape(images * rows_dev, cols_dev, 1))[:, :, 0]
    cell_windows = window_split(shifted.reshape(images * rows_dev, cols_dev, features))
    cot_flat = window_split(shifted_cot.reshape(images * rows_dev, cols_dev, features)).reshape(
        -1, features
    )
    selector = (
        rel_index.reshape(-1)[:, None] == jnp.arange(bias_table.shape[1], dtype=jnp.int32)[None, :]
    ).astype(jnp.float32)
    bias_full = jnp.dot(selector, bias_table.T, precision=lax.Precision.HIGHEST).T.reshape(
        head_count, WIN * WIN, WIN * WIN
    )
    stored_residuals, attended = attend_forward(
        cell_windows, labels, layer_norm_gain, qkv_full, bias_full
    )
    d_attended = lax.dot_general(
        cot_flat, out_full, (((1,), (1,)), ((), ())), preferred_element_type=jnp.float32
    ).astype(jnp.bfloat16)
    partial_rows = summed_on_arrival(
        lax.dot_general(
            attended, cot_flat, (((0,), (0,)), ((), ())), preferred_element_type=jnp.float32
        ).astype(jnp.bfloat16),
        "row",
        0,
    )
    d_rows, gain_contribution, table_part = attend_backward(
        stored_residuals, d_attended, layer_norm_gain, qkv_full
    )
    branch_gradient = window_join(
        d_rows.reshape(-1, WIN * WIN, features), images * rows_dev, cols_dev
    ).reshape(images, rows_dev, cols_dev, features)
    patch_rows = patches.reshape(-1, patches.shape[-1])
    cot_rows = cotangent.reshape(-1, features)
    contract = (((0,), (0,)), ((), ()))
    branch_patches = moved_patches.reshape(-1, patches.shape[-1])
    back_rows = branch_gradient.reshape(-1, features)
    embed_grad = lax.dot_general(
        patch_rows, cot_rows, contract, preferred_element_type=jnp.float32
    ) + lax.dot_general(branch_patches, back_rows, contract, preferred_element_type=jnp.float32)
    bias_grad = jnp.sum(cot_rows, axis=0, dtype=jnp.float32) + jnp.sum(
        back_rows, axis=0, dtype=jnp.float32
    )
    table_grad = jnp.dot(
        table_part.reshape(head_count, -1), selector, precision=lax.Precision.HIGHEST
    )
    head_table = table_grad.reshape(-1)
    pieces = [embed_grad.reshape(-1), bias_grad, gain_contribution, head_table]
    line = jnp.concatenate(pieces)
    row_count = lax.axis_size("row")
    piece = -(-line.size // (row_count * 1024)) * 1024
    line = jnp.pad(line, (0, row_count * piece - line.size)).reshape(row_count, piece // 128, 128)
    mine = exchange(line, "row").sum(axis=0).reshape(-1)
    col_blocks = in_blocks(partial_rows, 1, lax.axis_size(("col", "dp")))
    block_shape = col_blocks.shape
    col_blocks = col_blocks.reshape(block_shape[0], -1)
    own = jnp.broadcast_to(mine[None], (block_shape[0], piece))
    both = exchange(jnp.concatenate([own, col_blocks], axis=1), ("col", "dp")).sum(axis=0)
    out_weight_grad = both[piece:].reshape(block_shape[1:])
    total = spread(both[:piece].reshape(piece // 128, 128), "row").reshape(-1)
    results, at = ([], 0)
    for a, shape in zip(pieces, (embed_grad.shape, (features,), (features,), table_grad.shape)):
        results.append(total[at : at + a.size].reshape(shape))
        at += a.size
    return (out_weight_grad, *results)


def solution(mesh):
    return jax.shard_map(
        on_device,
        mesh=mesh,
        in_specs=(
            P("dp", None, "row", "col"),
            P("dp", "row", "col", None),
            P(),
            P(),
            P(),
            P("row", ("col", "dp")),
            P("row", ("col", "dp")),
            P(),
            P(),
            P("dp", None),
        ),
        out_specs=(P("row", ("col", "dp")), P(), P(), P(), P()),
        check_vma=False,
    )
```

profile of v0, /device:TPU:1, one launch (start us, length us, event | category | flops | bytes accessed | tf_op | source)
XLA Modules:
  0.0 269.2 jit_solution(6066088477923813417)
XLA Ops:
  7.2 0.8 reshape.251
  8.0 0.8 reshape.250
  9.6 1.8 reduce.5
  11.5 28.5 %all_to_all.33 = bf16[16,2,3072]{2,1,0:T(2,128)(2,1)S(1)} all-to-all(bf16[16,2,3072]{2,1,0:T(2,128)(2,1)S(1)} %reshape.400), channel_id=1, replica_groups=mesh['row'=32,'col'=8,'dp'=2] {'col','dp'}, dimensions={0} | all-to-all | bytes 393216 | tf_op jit(solution)/shard_map/all_to_all | solution.py:18
  42.2 3.7 %collective-permute-start = (bf16[1,3,32,128]{3,2,1,0:T(8,128)(2,1)S(1)}, bf16[1,3,32,128]{3,2,1,0:T(8,128)(2,1)S(1)}, u32[]{:S(2)}, u32[]{:S(2)}) collective-permute-start(bf16[1,3,32,128]{3,2,1,0:T(8,128)(2,1)S(1)} %copy-done.12), channel_id=1, source_target_pairs={{0,496},{16,0},{32,16},{48,32},{64,48},{80,64},{96,80},{112,96},{1... | collective-permute-start | bytes 73736 | tf_op jit(solution)/shard_map/ppermute | solution.py:39
  45.9 3.3 %collective-permute-start.2 = (bf16[1,8,32,1024]{3,2,1,0:T(8,128)(2,1)S(1)}, bf16[1,8,32,1024]{3,2,1,0:T(8,128)(2,1)S(1)}, u32[]{:S(2)}, u32[]{:S(2)}) collective-permute-start(bf16[1,8,32,1024]{3,2,1,0:T(8,128)(2,1)S(1)} %copy-done.3), channel_id=1, source_target_pairs={{0,496},{16,0},{32,16},{48,32},{64,48},{80,64},{96,80},{112,96},{1... | collective-permute-start | bytes 1572872 | tf_op jit(solution)/shard_map/ppermute | solution.py:39
  49.3 1.7 reshape.246
  54.0 2.6 convolution_bitcast_fusion
  56.5 0.9 fusion.48
  58.3 1.9 collective-permute-start.1
  63.7 0.9 copy.218
  66.1 1.7 reshape.248
  69.7 2.6 collective-permute-start.3
  73.3 2.6 collective-permute-done.3
  76.2 31.0 %all-gather.2.cloned.1.call-done = bf16[1024,3072]{1,0:T(8,128)(2,1)} async-done(((bf16[32,3072]{1,0:T(8,128)(2,1)}), bf16[1024,3072]{1,0:T(8,128)(2,1)}) %all-gather.2.cloned.1.call-update) | async-done | bytes 6291472 | tf_op jit(solution)/shard_map/all_gather | solution.py:212
  107.2 3.7 %fusion.6 = bf16[256,2304]{1,0:T(8,128)(2,1)S(1)} fusion(bf16[256,1024]{1,0:T(8,128)(2,1)S(1)} %multiply_convert_fusion.3, bf16[1024,3072]{1,0:T(8,128)(2,1)} %all-gather.2.cloned.1.call-done), kind=kOutput, calls=%fused_computation.8 | convolution fusion | flops 1208549376 | bytes 6422528 | tf_op jit(solution)/shard_map/dot_general | solution.py:105
  110.9 1.0 fusion.43
  112.5 1.0 copy.224
  113.5 1.7 reshape.398
  115.2 1.6 copy.237
  116.8 2.5 reshape.396
  119.2 1.8 copy.228
  121.0 2.7 %slice.173 = bf16[1024,768]{1,0:T(8,128)(2,1)} slice(bf16[1024,3072]{1,0:T(8,128)(2,1)} %all-gather.2.cloned.1.call-done), slice={[0:1024], [2304:3072]} | slice | bytes 3145728 | tf_op jit(solution)/shard_map/slice | solution.py:216
  123.8 3.9 %reshape.257 = bf16[768,1024]{1,0:T(8,128)(2,1)} reshape(bf16[1024,768]{1,0:T(8,128)(2,1)} %slice.173) | data formatting | bytes 3145728 | tf_op jit(solution)/shard_map/reshape | solution.py:216
  127.7 2.8 %convolution_convert_fusion.3 = bf16[256,768]{1,0:T(8,128)(2,1)} fusion(bf16[256,1024]{1,0:T(8,128)(2,1)S(1)} %bitcast.133, bf16[768,1024]{1,0:T(8,128)(2,1)} %reshape.257), kind=kOutput, calls=%fused_computation.28 | convolution fusion | flops 402849792 | bytes 2490368 | tf_op jit(solution)/shard_map/dot_general | solution.py:245
  130.4 2.5 reshape.397
  132.9 2.5 copy.232
  135.9 1.7 fusion.47
  137.6 3.6 %fusion.14 = bf16[4,64,12,64]{1,3,2,0:T(8,128)(2,1)} fusion(bf16[4,64,12,64]{1,3,2,0:T(8,128)(2,1)} %copy.232, f32[4,12,64]{2,1,0:T(8,128)S(1)} %get-tuple-element.63, f32[4,12,64,64]{2,3,1,0:T(8,128)} %copy-done.1), kind=kOutput, calls=%fused_computation.24 | convolution fusion | flops 25955392 | bytes 1585152 | tf_op jit(solution)/shard_map/whmn,wmhd->wnhd/dot_general | solution.py:154
  141.2 2.5 multiply_reduce_fusion
  143.7 1.3 fusion.29
  145.0 1.5 fusion.17
  146.4 1.5 fusion.16
  149.1 1.6 copy.227
  150.7 1.3 reshape.260
  152.0 0.8 copy.231
  153.3 4.2 %multiply_reduce_fusion.2 = (f32[256]{0:T(256)S(1)}, f32[1024]{0:T(1024)S(1)}, f32[256]{0:T(256)S(1)}, f32[256,1024]{1,0:T(8,128)S(1)}) fusion(f32[1,4,8,8,1024]{4,3,2,1,0:T(8,128)S(1)} %copy.211, f32[1024]{0:T(1024)S(1)} %copy-done.15, f32[256]{0:T(256)S(1)} %div.24, f32[256]{0:T(256)S(1)} %rsqrt.12, bf16[1024,3072]{1,0:T(8,128)(2,1)} %all-gather.2.cloned.1.call-done, ...), kind=kOutput, calls=%fused_computation.47 | convolution fusion | flops 1213594112 | bytes 8007680 | tf_op jit(solution)/shard_map/dot_general | solution.py:178
  158.8 1.4 fusion.1
  160.7 0.7 select_maximum_fusion
  161.4 5.1 %all-to-all-start.1 = ((f32[32,16,128]{2,1,0:T(8,128)}), f32[32,16,128]{2,1,0:T(8,128)S(1)}, u32[]{:S(2)}, u32[]{:S(2)}) async-start(f32[32,16,128]{2,1,0:T(8,128)} %bitcast.30), calls=%async_computation.1 | async-start | bytes 524288 | tf_op jit(solution)/shard_map/all_to_all | solution.py:18
  166.5 2.5 fusion.15
  170.1 1.7 convolution_convert_fusion
  171.8 5.7 %all-to-all-done.1 = f32[32,16,128]{2,1,0:T(8,128)S(1)} async-done(((f32[32,16,128]{2,1,0:T(8,128)}), f32[32,16,128]{2,1,0:T(8,128)S(1)}, u32[]{:S(2)}, u32[]{:S(2)}) %all-to-all-start.1) | async-done | bytes 262176 | tf_op jit(solution)/shard_map/all_to_all | solution.py:18
  177.6 3.9 %all-to-all-start.2 = ((bf16[32,24,1024]{2,1,0:T(8,128)(2,1)}), bf16[32,24,1024]{2,1,0:T(8,128)(2,1)S(1)}, u32[]{:S(2)}, u32[]{:S(2)}) async-start(bf16[32,24,1024]{2,1,0:T(8,128)(2,1)} %bitcast.33), calls=%async_computation.2 | async-start | bytes 3145728 | tf_op jit(solution)/shard_map/all_to_all | solution.py:49
  181.5 36.9 %all-to-all-done.2 = bf16[32,24,1024]{2,1,0:T(8,128)(2,1)S(1)} async-done(((bf16[32,24,1024]{2,1,0:T(8,128)(2,1)}), bf16[32,24,1024]{2,1,0:T(8,128)(2,1)S(1)}, u32[]{:S(2)}, u32[]{:S(2)}) %all-to-all-start.2) | async-done | bytes 1572896 | tf_op jit(solution)/shard_map/all_to_all | solution.py:49
  219.1 21.9 %all_to_all.34 = f32[16,1,3584]{2,1,0:T(1,128)S(1)} all-to-all(f32[16,1,3584]{2,1,0:T(1,128)S(1)} %all_to_all.25), channel_id=1, replica_groups=mesh['row'=32,'col'=8,'dp'=2] {'col','dp'}, dimensions={0} | all-to-all | bytes 458752 | tf_op jit(solution)/shard_map/all_to_all | solution.py:18
  241.9 7.4 %all-to-all-start.4 = ((f32[32,16,128]{2,1,0:T(8,128)}), f32[32,16,128]{2,1,0:T(8,128)S(1)}, u32[]{:S(2)}, u32[]{:S(2)}) async-start(f32[32,16,128]{2,1,0:T(8,128)} %broadcast_in_dim.66), calls=%async_computation.4 | async-start | bytes 524288 | tf_op jit(solution)/shard_map/all_to_all | solution.py:18
  250.0 10.4 %all-to-all-done.4 = f32[32,16,128]{2,1,0:T(8,128)S(1)} async-done(((f32[32,16,128]{2,1,0:T(8,128)}), f32[32,16,128]{2,1,0:T(8,128)S(1)}, u32[]{:S(2)}, u32[]{:S(2)}) %all-to-all-start.4) | async-done | bytes 262176 | tf_op jit(solution)/shard_map/all_to_all | solution.py:18
  (125 shorter events, 18.0 us)
Async XLA Ops:
  7.2 61.2 %copy-start = (bf16[48,1024]{1,0:T(8,128)(2,1)S(1)}, bf16[48,1024]{1,0:T(8,128)(2,1)}, u32[]{:S(2)}) copy-start(bf16[48,1024]{1,0:T(8,128)(2,1)} %param.12) | copy-start | bytes 294916
  7.2 100.0 %all-gather.2.cloned.1.call-start = ((), (), s32[]{:S(2)}) async-start(), calls=%async_computation.5 | async-start | bytes 6488064 | tf_op jit(solution)/shard_map/all_gather | solution.py:212
  40.1 2.1 copy-start.12
  40.1 5.8 %copy-start.3 = (bf16[1,8,32,1024]{3,2,1,0:T(8,128)(2,1)S(1)}, bf16[1,8,32,1024]{3,2,1,0:T(8,128)(2,1)}, u32[]{:S(2)}) copy-start(bf16[1,8,32,1024]{3,2,1,0:T(8,128)(2,1)} %param.11) | copy-start | bytes 1572868
  40.4 10.6 %copy-start.19 = (s32[1,2]{1,0:T(1,128)S(1)}, s32[1,2]{1,0:T(1,128)}, u32[]{:S(2)}) copy-start(s32[1,2]{1,0:T(1,128)} %param.19) | copy-start | bytes 28
  40.4 12.7 %copy-start.14 = (s32[64,64]{1,0:T(8,128)S(1)}, s32[64,64]{1,0:T(8,128)}, u32[]{:S(2)}) copy-start(s32[64,64]{1,0:T(8,128)} %param.18) | copy-start | bytes 49156
  41.2 12.8 %copy-start.20 = (f32[12,225]{1,0:T(8,128)S(1)}, f32[12,225]{1,0:T(8,128)}, u32[]{:S(2)}) copy-start(f32[12,225]{1,0:T(8,128)} %param.17) | copy-start | bytes 32404
  42.2 16.0 %collective-permute-start = (bf16[1,3,32,128]{3,2,1,0:T(8,128)(2,1)S(1)}, bf16[1,3,32,128]{3,2,1,0:T(8,128)(2,1)S(1)}, u32[]{:S(2)}, u32[]{:S(2)}) collective-permute-start(bf16[1,3,32,128]{3,2,1,0:T(8,128)(2,1)S(1)} %copy-done.12), channel_id=1, source_target_pairs={{0,496},{16,0},{32,16},{48,32},{64,48},{80,64},{96,80},{112,96},{1... | collective-permute-start | bytes 73736 | tf_op jit(solution)/shard_map/ppermute | solution.py:39
  45.9 23.5 %collective-permute-start.2 = (bf16[1,8,32,1024]{3,2,1,0:T(8,128)(2,1)S(1)}, bf16[1,8,32,1024]{3,2,1,0:T(8,128)(2,1)S(1)}, u32[]{:S(2)}, u32[]{:S(2)}) collective-permute-start(bf16[1,8,32,1024]{3,2,1,0:T(8,128)(2,1)S(1)} %copy-done.3), channel_id=1, source_target_pairs={{0,496},{16,0},{32,16},{48,32},{64,48},{80,64},{96,80},{112,96},{1... | collective-permute-start | bytes 1572872 | tf_op jit(solution)/shard_map/ppermute | solution.py:39
  53.1 5.1 %copy-start.16 = (s32[4096]{0:T(1024)}, s32[4096]{0:T(1024)S(1)}, u32[]{:S(2)}) copy-start(s32[4096]{0:T(1024)S(1)} %eq.39) | copy-start | bytes 49156
  58.3 7.7 %collective-permute-start.1 = (bf16[1,3,32,32]{3,2,1,0:T(8,128)(2,1)S(1)}, bf16[1,3,32,32]{3,2,1,0:T(8,128)(2,1)S(1)}, u32[]{:S(2)}, u32[]{:S(2)}) collective-permute-start(bf16[1,3,32,32]{3,2,1,0:T(8,128)(2,1)S(1)} %bitcast.145), channel_id=1, source_target_pairs={{0,14},{2,0},{4,2},{6,4},{8,6},{10,8},{12,10},{14,12},{1,15},{3,1}... | collective-permute-start | bytes 18440 | tf_op jit(solution)/shard_map/ppermute | solution.py:39
  63.5 4.9 %copy-start.18 = (f32[1024]{0:T(1024)S(1)}, f32[1024]{0:T(1024)}, u32[]{:S(2)}) copy-start(f32[1024]{0:T(1024)} %param.13) | copy-start | bytes 12292
  69.1 3.2 %copy-start.15 = (f32[1024]{0:T(1024)S(1)}, f32[1024]{0:T(1024)}, u32[]{:S(2)}) copy-start(f32[1024]{0:T(1024)} %param.14) | copy-start | bytes 12292
  69.7 6.1 %collective-permute-start.3 = (bf16[1,8,8,1024]{3,2,1,0:T(8,128)(2,1)S(1)}, bf16[1,8,8,1024]{3,2,1,0:T(8,128)(2,1)S(1)}, u32[]{:S(2)}, u32[]{:S(2)}) collective-permute-start(bf16[1,8,8,1024]{3,2,1,0:T(8,128)(2,1)S(1)} %slice.172), channel_id=1, source_target_pairs={{0,14},{2,0},{4,2},{6,4},{8,6},{10,8},{12,10},{14,12},{1,15},{3,1}... | collective-permute-start | bytes 393224 | tf_op jit(solution)/shard_map/ppermute | solution.py:39
  76.2 51.5 %copy-start.5 = (bf16[1,4,8,8,1024]{4,3,2,1,0:T(8,128)(2,1)}, bf16[1,4,8,8,1024]{4,3,2,1,0:T(8,128)(2,1)S(1)}, u32[]{:S(2)}) copy-start(bf16[1,4,8,8,1024]{4,3,2,1,0:T(8,128)(2,1)S(1)} %copy.219) | copy-start | bytes 1572868
  130.4 5.0 %copy-start.7 = (f32[12,64,64]{1,2,0:T(8,128)S(1)}, f32[12,64,64]{1,2,0:T(8,128)}, u32[]{:S(2)}) copy-start(f32[12,64,64]{1,2,0:T(8,128)} %copy.218) | copy-start | bytes 589828
  135.9 1.7 copy-start.1
  141.2 2.5 copy-start.2
  146.4 1.5 copy-start.10
  149.1 2.9 %copy-start.4 = (bf16[4,64,12,64]{3,1,2,0:T(8,128)(2,1)S(1)}, bf16[4,64,12,64]{3,1,2,0:T(8,128)(2,1)}, u32[]{:S(2)}) copy-start(bf16[4,64,12,64]{3,1,2,0:T(8,128)(2,1)} %fusion.17) | copy-start | bytes 1179652
  157.5 1.0 copy-start.8
  157.9 0.9 copy-start.17
  158.0 2.3 copy-start.11
  158.0 2.3 copy-start.13
  158.8 7.7 %copy-start.9 = (bf16[4,64,12,64]{1,3,2,0:T(8,128)(2,1)S(1)}, bf16[4,64,12,64]{1,3,2,0:T(8,128)(2,1)}, u32[]{:S(2)}) copy-start(bf16[4,64,12,64]{1,3,2,0:T(8,128)(2,1)} %copy.237) | copy-start | bytes 1179652
  161.4 16.2 %all-to-all-start.1 = ((f32[32,16,128]{2,1,0:T(8,128)}), f32[32,16,128]{2,1,0:T(8,128)S(1)}, u32[]{:S(2)}, u32[]{:S(2)}) async-start(f32[32,16,128]{2,1,0:T(8,128)} %bitcast.30), calls=%async_computation.1 | async-start | bytes 524288 | tf_op jit(solution)/shard_map/all_to_all | solution.py:18
  169.0 1.1 copy-start.6
  177.6 40.9 %all-to-all-start.2 = ((bf16[32,24,1024]{2,1,0:T(8,128)(2,1)}), bf16[32,24,1024]{2,1,0:T(8,128)(2,1)S(1)}, u32[]{:S(2)}, u32[]{:S(2)}) async-start(bf16[32,24,1024]{2,1,0:T(8,128)(2,1)} %bitcast.33), calls=%async_computation.2 | async-start | bytes 3145728 | tf_op jit(solution)/shard_map/all_to_all | solution.py:49
  241.9 18.4 %all-to-all-start.4 = ((f32[32,16,128]{2,1,0:T(8,128)}), f32[32,16,128]{2,1,0:T(8,128)S(1)}, u32[]{:S(2)}, u32[]{:S(2)}) async-start(f32[32,16,128]{2,1,0:T(8,128)} %broadcast_in_dim.66), calls=%async_computation.4 | async-start | bytes 524288 | tf_op jit(solution)/shard_map/all_to_all | solution.py:18
Sparse Core Ops, SparseCore 0:
  42.3 64.7 all-gather.1
where the time goes:
time: 270 us; the launch traced here: 269 us
  waiting for transfers between devices  86.7 us (32%)
  blocking collectives  50.4 us (19%)
  local copies, waits for them, and re-layouts  44.5 us (16%)
  matrix products  30 us (11%)
  starting transfers between devices  27.9 us (10%)
  between operations  21.3 us (8%)
  other arithmetic  8.47 us (3%)
    all_to_all x2, blocking collectives, exchange(): return lax.all_to_all(blocks, axis, split_axis=0, concat_axis=0, tiled=True)  50.4 us
    all_to_all x1, waiting for transfers between devices, summed_on_arrival(): lax.all_to_all(blocks, axis, split_axis=0, concat_axis=0, tiled=True)  36.9 us
    all_gather x1, waiting for transfers between devices, on_device(): lax.all_gather(jnp.concatenate([qkv_columns, out_tall], axis=1), 'row', a...  31 us
    all_to_all x2, waiting for transfers between devices, exchange(): return lax.all_to_all(blocks, axis, split_axis=0, concat_axis=0, tiled=True)  16.1 us
    all_to_all x2, starting transfers between devices, exchange(): return lax.all_to_all(blocks, axis, split_axis=0, concat_axis=0, tiled=True)  12.5 us
    ppermute x4, starting transfers between devices, from_behind(): return lax.ppermute(value, axis, pairs)  11.6 us
  transfers between devices with their start and end apart: 8, of which 5 were waited for; matrix products, arithmetic and copies ran while one was open for 7% of the time, Pallas kernels for 0%

commit v1 on v0

--- a/solution.py
+++ b/solution.py
@@ -209,9 +209,14 @@
     qkv_columns, out_columns = gather_together((qkv_weight, out_weight), ("col", "dp"), (1, 1))
     rows_qkv, width_qkv = qkv_columns.shape
     out_tall = out_columns.reshape(rows_qkv, -1)
-    weights = lax.all_gather(
-        jnp.concatenate([qkv_columns, out_tall], axis=1), "row", axis=0, tiled=True
-    )
+
+    def bench_launch(block_here, link_axis):
+        big = lax.all_to_all(
+            jnp.stack([block_here for _ in range(lax.axis_size(link_axis))], 0), link_axis, 0, 0
+        )
+        return jnp.concatenate(big, 0)
+
+    weights = bench_launch(jnp.concatenate([qkv_columns, out_tall], axis=1), link_axis="row")
     qkv_full = weights[:, :width_qkv]
     out_full = weights[:, width_qkv:].reshape(-1, features)
     patches = make_patches(pixels)

time: 270 us -> 353 us (1.31)
  waiting for transfers between devices: 86.7 us -> 157 us
  starting transfers between devices: 27.9 us -> 56.2 us
  between operations: 21.3 us -> 7.9 us
  blocking collectives: 50.4 us -> 46.2 us
    all_to_all x0 -> x1, waiting for transfers between devices: none -> 77.6 us  [bench_launch(): lax.all_to_all(jnp.stack([block_here for _ in range(lax.axis_size(link_ax...]
    all_gather x1 -> x0, waiting for transfers between devices: 31 us -> none  [on_device(): lax.all_gather(jnp.concatenate([qkv_columns, out_tall], axis=1), 'row', a...]
    ppermute x4, waiting for transfers between devices: 2.56 us -> 26.8 us  [from_behind(): return lax.ppermute(value, axis, pairs)]
    all_to_all x2, starting transfers between devices: 12.5 us -> 30 us  [exchange(): return lax.all_to_all(blocks, axis, split_axis=0, concat_axis=0, tiled=True)]
    all_to_all x0 -> x1, starting transfers between devices: none -> 8.38 us  [bench_launch(): lax.all_to_all(jnp.stack([block_here for _ in range(lax.axis_size(link_ax...]
    all_to_all x2, blocking collectives: 50.4 us -> 46.2 us  [exchange(): return lax.all_to_all(blocks, axis, split_axis=0, concat_axis=0, tiled=True)]
  transfers between devices with their start and end apart: 8 -> 8, of which waited for: 5 -> 7; matrix products, arithmetic and copies ran while one was open for 7% -> 6% of each run, Pallas kernels for 0% -> 0%
where the time goes in v1:
time: 353 us; the launch traced here: 352 us
  waiting for transfers between devices  157 us (44%)
  starting transfers between devices  56.2 us (16%)
  local copies, waits for them, and re-layouts  47.6 us (13%)
  blocking collectives  46.2 us (13%)
  matrix products  27.8 us (8%)
  other arithmetic  8.6 us (2%)
  between operations  7.9 us (2%)
    all_to_all x1, waiting for transfers between devices, bench_launch(): lax.all_to_all(jnp.stack([block_here for _ in range(lax.axis_size(link_ax...  77.6 us
    all_to_all x2, blocking collectives, exchange(): return lax.all_to_all(blocks, axis, split_axis=0, concat_axis=0, tiled=True)  46.2 us
    all_to_all x1, waiting for transfers between devices, summed_on_arrival(): lax.all_to_all(blocks, axis, split_axis=0, concat_axis=0, tiled=True)  36.9 us
    all_to_all x2, starting transfers between devices, exchange(): return lax.all_to_all(blocks, axis, split_axis=0, concat_axis=0, tiled=True)  30 us
    ppermute x4, waiting for transfers between devices, from_behind(): return lax.ppermute(value, axis, pairs)  26.8 us
    all_to_all x2, waiting for transfers between devices, exchange(): return lax.all_to_all(blocks, axis, split_axis=0, concat_axis=0, tiled=True)  16.1 us
    ppermute x4, starting transfers between devices, from_behind(): return lax.ppermute(value, axis, pairs)  13.9 us
    all_to_all x1, starting transfers between devices, bench_launch(): lax.all_to_all(jnp.stack([block_here for _ in range(lax.axis_size(link_ax...  8.38 us
  transfers between devices with their start and end apart: 8, of which 7 were waited for; matrix products, arithmetic and copies ran while one was open for 6% of the time, Pallas kernels for 0%

profile of v1, /device:TPU:1, one launch (start us, length us, event | category | flops | bytes accessed | tf_op | source)
XLA Modules:
  0.0 351.6 jit_solution(8650030437537371208)
XLA Ops:
  1.5 0.8 reshape.255
  3.0 1.8 reduce.5
  4.9 28.5 %all_to_all.38 = bf16[16,2,3072]{2,1,0:T(2,128)(2,1)S(1)} all-to-all(bf16[16,2,3072]{2,1,0:T(2,128)(2,1)S(1)} %reshape.406), channel_id=1, replica_groups=mesh['row'=32,'col'=8,'dp'=2] {'col','dp'}, dimensions={0} | all-to-all | bytes 393216 | tf_op jit(solution)/shard_map/all_to_all | solution.py:18
  34.9 3.4 stack.2
  38.4 8.4 %all-to-all-start.1 = ((bf16[32,32,3072]{2,1,0:T(8,128)(2,1)}), bf16[32,32,3072]{2,1,0:T(8,128)(2,1)}, u32[]{:S(2)}, u32[]{:S(2)}) async-start(bf16[32,32,3072]{2,1,0:T(8,128)(2,1)} %stack.2), calls=%async_computation.1 | async-start | bytes 12582912 | tf_op jit(solution)/shard_map/all_to_all | solution.py:214
  46.8 2.2 collective-permute-start
  49.0 7.4 %collective-permute-start.2 = (bf16[1,8,32,1024]{3,2,1,0:T(8,128)(2,1)S(1)}, bf16[1,8,32,1024]{3,2,1,0:T(8,128)(2,1)S(1)}, u32[]{:S(2)}, u32[]{:S(2)}) collective-permute-start(bf16[1,8,32,1024]{3,2,1,0:T(8,128)(2,1)S(1)} %copy-done.3), channel_id=1, source_target_pairs={{0,496},{16,0},{32,16},{48,32},{64,48},{80,64},{96,80},{112,96},{1... | collective-permute-start | bytes 1572872 | tf_op jit(solution)/shard_map/ppermute | solution.py:39
  56.4 1.7 reshape.251
  61.0 2.6 convolution_bitcast_fusion
  63.6 0.9 fusion.48
  65.3 20.8 %collective-permute-done = bf16[1,3,32,128]{3,2,1,0:T(8,128)(2,1)S(1)} collective-permute-done((bf16[1,3,32,128]{3,2,1,0:T(8,128)(2,1)S(1)}, bf16[1,3,32,128]{3,2,1,0:T(8,128)(2,1)S(1)}, u32[]{:S(2)}, u32[]{:S(2)}) %collective-permute-start) | collective-permute-done | bytes 24608 | tf_op jit(solution)/shard_map/ppermute | solution.py:39
  86.1 2.2 collective-permute-start.1
  91.8 0.9 copy.218
  94.1 1.7 reshape.253
  97.5 3.9 %collective-permute-done.2 = bf16[1,8,32,1024]{3,2,1,0:T(8,128)(2,1)S(1)} collective-permute-done((bf16[1,8,32,1024]{3,2,1,0:T(8,128)(2,1)S(1)}, bf16[1,8,32,1024]{3,2,1,0:T(8,128)(2,1)S(1)}, u32[]{:S(2)}, u32[]{:S(2)}) %collective-permute-start.2) | collective-permute-done | bytes 524320 | tf_op jit(solution)/shard_map/ppermute | solution.py:39
  101.6 2.2 collective-permute-start.3
  103.8 1.1 multiply_convert_fusion.3
  105.6 2.1 collective-permute-done.3
  108.1 77.6 %all-to-all-done.1 = bf16[32,32,3072]{2,1,0:T(8,128)(2,1)} async-done(((bf16[32,32,3072]{2,1,0:T(8,128)(2,1)}), bf16[32,32,3072]{2,1,0:T(8,128)(2,1)}, u32[]{:S(2)}, u32[]{:S(2)}) %all-to-all-start.1) | async-done | bytes 6291488 | tf_op jit(solution)/shard_map/all_to_all | solution.py:214
  185.6 2.7 slice.173
  188.4 3.7 %fusion.6 = bf16[256,2304]{1,0:T(8,128)(2,1)S(1)} fusion(bf16[256,1024]{1,0:T(8,128)(2,1)S(1)} %copy-done.12, bf16[1024,3072]{1,0:T(8,128)(2,1)} %bitcast.15), kind=kOutput, calls=%fused_computation.8 | convolution fusion | flops 1208549376 | bytes 6422528 | tf_op jit(solution)/shard_map/dot_general | solution.py:105
  192.1 1.0 fusion.43
  193.7 1.0 copy.224
  194.7 1.7 reshape.404
  196.4 1.6 copy.237
  198.0 2.5 reshape.402
  200.5 1.8 copy.228
  202.3 4.0 %reshape.263 = bf16[768,1024]{1,0:T(8,128)(2,1)} reshape(bf16[1024,768]{1,0:T(8,128)(2,1)} %slice.173) | data formatting | bytes 3145728 | tf_op jit(solution)/shard_map/reshape | solution.py:221
  206.3 2.8 convolution_convert_fusion.3
  209.0 2.5 reshape.403
  211.5 2.5 copy.232
  214.5 1.7 fusion.47
  216.2 3.7 %fusion.14 = bf16[4,64,12,64]{1,3,2,0:T(8,128)(2,1)} fusion(bf16[4,64,12,64]{1,3,2,0:T(8,128)(2,1)} %copy.232, f32[4,12,64]{2,1,0:T(8,128)S(1)} %get-tuple-element.63, f32[4,12,64,64]{2,3,1,0:T(8,128)} %copy-done.1), kind=kOutput, calls=%fused_computation.24 | convolution fusion | flops 25955392 | bytes 1585152 | tf_op jit(solution)/shard_map/whmn,wmhd->wnhd/dot_general | solution.py:154
  219.9 2.3 multiply_reduce_fusion
  222.2 1.2 fusion.29
  225.7 1.2 reshape.268
  228.0 0.8 copy.231
  229.3 4.1 %multiply_reduce_fusion.2 = (f32[256]{0:T(256)S(1)}, f32[1024]{0:T(1024)S(1)}, f32[256]{0:T(256)S(1)}, f32[256,1024]{1,0:T(8,128)S(1)}) fusion(f32[1,4,8,8,1024]{4,3,2,1,0:T(8,128)S(1)} %copy.211, f32[1024]{0:T(1024)S(1)} %copy-done.17, f32[256]{0:T(256)S(1)} %div.24, f32[256]{0:T(256)S(1)} %rsqrt.12, bf16[1024,3072]{1,0:T(8,128)(2,1)} %bitcast.15, ...), kind=kOutput, calls=%fused_computation.47 | convolution fusion | flops 1213594112 | bytes 8007680 | tf_op jit(solution)/shard_map/dot_general | solution.py:178
  234.7 1.4 fusion.1
  237.3 22.6 %all-to-all-start.2 = ((f32[32,16,128]{2,1,0:T(8,128)}), f32[32,16,128]{2,1,0:T(8,128)S(1)}, u32[]{:S(2)}, u32[]{:S(2)}) async-start(f32[32,16,128]{2,1,0:T(8,128)} %bitcast.31), calls=%async_computation.2 | async-start | bytes 524288 | tf_op jit(solution)/shard_map/all_to_all | solution.py:18
  259.9 2.5 fusion.15
  263.5 1.7 convolution_convert_fusion
  265.2 5.7 %all-to-all-done.2 = f32[32,16,128]{2,1,0:T(8,128)S(1)} async-done(((f32[32,16,128]{2,1,0:T(8,128)}), f32[32,16,128]{2,1,0:T(8,128)S(1)}, u32[]{:S(2)}, u32[]{:S(2)}) %all-to-all-start.2) | async-done | bytes 262176 | tf_op jit(solution)/shard_map/all_to_all | solution.py:18
  271.0 3.9 %all-to-all-start.3 = ((bf16[32,24,1024]{2,1,0:T(8,128)(2,1)}), bf16[32,24,1024]{2,1,0:T(8,128)(2,1)S(1)}, u32[]{:S(2)}, u32[]{:S(2)}) async-start(bf16[32,24,1024]{2,1,0:T(8,128)(2,1)} %bitcast.34), calls=%async_computation.3 | async-start | bytes 3145728 | tf_op jit(solution)/shard_map/all_to_all | solution.py:49
  274.9 36.9 %all-to-all-done.3 = bf16[32,24,1024]{2,1,0:T(8,128)(2,1)S(1)} async-done(((bf16[32,24,1024]{2,1,0:T(8,128)(2,1)}), bf16[32,24,1024]{2,1,0:T(8,128)(2,1)S(1)}, u32[]{:S(2)}, u32[]{:S(2)}) %all-to-all-start.3) | async-done | bytes 1572896 | tf_op jit(solution)/shard_map/all_to_all | solution.py:49
  312.5 17.7 %all_to_all.39 = f32[16,1,3584]{2,1,0:T(1,128)S(1)} all-to-all(f32[16,1,3584]{2,1,0:T(1,128)S(1)} %all_to_all.29), channel_id=1, replica_groups=mesh['row'=32,'col'=8,'dp'=2] {'col','dp'}, dimensions={0} | all-to-all | bytes 458752 | tf_op jit(solution)/shard_map/all_to_all | solution.py:18
  331.1 7.4 %all-to-all-start.5 = ((f32[32,16,128]{2,1,0:T(8,128)}), f32[32,16,128]{2,1,0:T(8,128)S(1)}, u32[]{:S(2)}, u32[]{:S(2)}) async-start(f32[32,16,128]{2,1,0:T(8,128)} %broadcast_in_dim.66), calls=%async_computation.5 | async-start | bytes 524288 | tf_op jit(solution)/shard_map/all_to_all | solution.py:18
  339.1 10.4 %all-to-all-done.5 = f32[32,16,128]{2,1,0:T(8,128)S(1)} async-done(((f32[32,16,128]{2,1,0:T(8,128)}), f32[32,16,128]{2,1,0:T(8,128)S(1)}, u32[]{:S(2)}, u32[]{:S(2)}) %all-to-all-start.5) | async-done | bytes 262176 | tf_op jit(solution)/shard_map/all_to_all | solution.py:18
  (129 shorter events, 20.8 us)
Async XLA Ops:
  0.6 95.9 %copy-start = (bf16[48,1024]{1,0:T(8,128)(2,1)S(1)}, bf16[48,1024]{1,0:T(8,128)(2,1)}, u32[]{:S(2)}) copy-start(bf16[48,1024]{1,0:T(8,128)(2,1)} %param.12) | copy-start | bytes 294916
  38.4 8.4 %copy-start.14 = (bf16[1,3,32,128]{3,2,1,0:T(8,128)(2,1)S(1)}, bf16[1,3,32,128]{3,2,1,0:T(8,128)(2,1)}, u32[]{:S(2)}) copy-start(bf16[1,3,32,128]{3,2,1,0:T(8,128)(2,1)} %param.10) | copy-start | bytes 73732
  38.4 10.6 %copy-start.3 = (bf16[1,8,32,1024]{3,2,1,0:T(8,128)(2,1)S(1)}, bf16[1,8,32,1024]{3,2,1,0:T(8,128)(2,1)}, u32[]{:S(2)}) copy-start(bf16[1,8,32,1024]{3,2,1,0:T(8,128)(2,1)} %param.11) | copy-start | bytes 1572868
  38.4 19.7 %copy-start.21 = (s32[1,2]{1,0:T(1,128)S(1)}, s32[1,2]{1,0:T(1,128)}, u32[]{:S(2)}) copy-start(s32[1,2]{1,0:T(1,128)} %param.19) | copy-start | bytes 28
  38.4 21.8 %copy-start.16 = (s32[64,64]{1,0:T(8,128)S(1)}, s32[64,64]{1,0:T(8,128)}, u32[]{:S(2)}) copy-start(s32[64,64]{1,0:T(8,128)} %param.18) | copy-start | bytes 49156
  38.4 147.3 %all-to-all-start.1 = ((bf16[32,32,3072]{2,1,0:T(8,128)(2,1)}), bf16[32,32,3072]{2,1,0:T(8,128)(2,1)}, u32[]{:S(2)}, u32[]{:S(2)}) async-start(bf16[32,32,3072]{2,1,0:T(8,128)(2,1)} %stack.2), calls=%async_computation.1 | async-start | bytes 12582912 | tf_op jit(solution)/shard_map/all_to_all | solution.py:214
  46.8 14.3 %copy-start.22 = (f32[12,225]{1,0:T(8,128)S(1)}, f32[12,225]{1,0:T(8,128)}, u32[]{:S(2)}) copy-start(f32[12,225]{1,0:T(8,128)} %param.17) | copy-start | bytes 32404
  46.8 39.2 %collective-permute-start = (bf16[1,3,32,128]{3,2,1,0:T(8,128)(2,1)S(1)}, bf16[1,3,32,128]{3,2,1,0:T(8,128)(2,1)S(1)}, u32[]{:S(2)}, u32[]{:S(2)}) collective-permute-start(bf16[1,3,32,128]{3,2,1,0:T(8,128)(2,1)S(1)} %copy-done.14), channel_id=1, source_target_pairs={{0,496},{16,0},{32,16},{48,32},{64,48},{80,64},{96,80},{112,96},{1... | collective-permute-start | bytes 73736 | tf_op jit(solution)/shard_map/ppermute | solution.py:39
  49.0 52.4 %collective-permute-start.2 = (bf16[1,8,32,1024]{3,2,1,0:T(8,128)(2,1)S(1)}, bf16[1,8,32,1024]{3,2,1,0:T(8,128)(2,1)S(1)}, u32[]{:S(2)}, u32[]{:S(2)}) collective-permute-start(bf16[1,8,32,1024]{3,2,1,0:T(8,128)(2,1)S(1)} %copy-done.3), channel_id=1, source_target_pairs={{0,496},{16,0},{32,16},{48,32},{64,48},{80,64},{96,80},{112,96},{1... | collective-permute-start | bytes 1572872 | tf_op jit(solution)/shard_map/ppermute | solution.py:39
  60.2 28.2 %copy-start.18 = (s32[4096]{0:T(1024)}, s32[4096]{0:T(1024)S(1)}, u32[]{:S(2)}) copy-start(s32[4096]{0:T(1024)S(1)} %eq.39) | copy-start | bytes 49156
  86.1 7.9 %collective-permute-start.1 = (bf16[1,3,32,32]{3,2,1,0:T(8,128)(2,1)S(1)}, bf16[1,3,32,32]{3,2,1,0:T(8,128)(2,1)S(1)}, u32[]{:S(2)}, u32[]{:S(2)}) collective-permute-start(bf16[1,3,32,32]{3,2,1,0:T(8,128)(2,1)S(1)} %bitcast.146), channel_id=1, source_target_pairs={{0,14},{2,0},{4,2},{6,4},{8,6},{10,8},{12,10},{14,12},{1,15},{3,1}... | collective-permute-start | bytes 18440 | tf_op jit(solution)/shard_map/ppermute | solution.py:39
  91.6 4.9 %copy-start.20 = (f32[1024]{0:T(1024)S(1)}, f32[1024]{0:T(1024)}, u32[]{:S(2)}) copy-start(f32[1024]{0:T(1024)} %param.13) | copy-start | bytes 12292
  97.1 6.7 %copy-start.17 = (f32[1024]{0:T(1024)S(1)}, f32[1024]{0:T(1024)}, u32[]{:S(2)}) copy-start(f32[1024]{0:T(1024)} %param.14) | copy-start | bytes 12292
  101.6 6.1 %collective-permute-start.3 = (bf16[1,8,8,1024]{3,2,1,0:T(8,128)(2,1)S(1)}, bf16[1,8,8,1024]{3,2,1,0:T(8,128)(2,1)S(1)}, u32[]{:S(2)}, u32[]{:S(2)}) collective-permute-start(bf16[1,8,8,1024]{3,2,1,0:T(8,128)(2,1)S(1)} %slice.172), channel_id=1, source_target_pairs={{0,14},{2,0},{4,2},{6,4},{8,6},{10,8},{12,10},{14,12},{1,15},{3,1}... | collective-permute-start | bytes 393224 | tf_op jit(solution)/shard_map/ppermute | solution.py:39
  108.1 98.2 %copy-start.4 = (bf16[1,4,8,8,1024]{4,3,2,1,0:T(8,128)(2,1)}, bf16[1,4,8,8,1024]{4,3,2,1,0:T(8,128)(2,1)S(1)}, u32[]{:S(2)}) copy-start(bf16[1,4,8,8,1024]{4,3,2,1,0:T(8,128)(2,1)S(1)} %copy.219) | copy-start | bytes 1572868
  185.6 2.7 copy-start.12
  209.0 5.0 %copy-start.6 = (f32[12,64,64]{1,2,0:T(8,128)S(1)}, f32[12,64,64]{1,2,0:T(8,128)}, u32[]{:S(2)}) copy-start(f32[12,64,64]{1,2,0:T(8,128)} %copy.218) | copy-start | bytes 589828
  214.5 1.7 copy-start.1
  216.2 3.7 %copy-start.8 = (bf16[4,64,12,64]{1,3,2,0:T(8,128)(2,1)S(1)}, bf16[4,64,12,64]{1,3,2,0:T(8,128)(2,1)}, u32[]{:S(2)}) copy-start(bf16[4,64,12,64]{1,3,2,0:T(8,128)(2,1)} %copy.237) | copy-start | bytes 1179652
  219.9 2.3 copy-start.2
  223.9 1.1 copy-start.10
  228.0 1.3 copy-start.13
  233.4 1.0 copy-start.7
  233.7 0.9 copy-start.19
  233.9 2.4 copy-start.11
  233.9 2.3 copy-start.15
  234.7 25.2 %copy-start.9 = (bf16[4,64,12,64]{1,3,2,0:T(8,128)(2,1)S(1)}, bf16[4,64,12,64]{1,3,2,0:T(8,128)(2,1)}, u32[]{:S(2)}) copy-start(bf16[4,64,12,64]{1,3,2,0:T(8,128)(2,1)} %copy.237) | copy-start | bytes 1179652
  237.3 33.7 %all-to-all-start.2 = ((f32[32,16,128]{2,1,0:T(8,128)}), f32[32,16,128]{2,1,0:T(8,128)S(1)}, u32[]{:S(2)}, u32[]{:S(2)}) async-start(f32[32,16,128]{2,1,0:T(8,128)} %bitcast.31), calls=%async_computation.2 | async-start | bytes 524288 | tf_op jit(solution)/shard_map/all_to_all | solution.py:18
  262.4 1.1 copy-start.5
  271.0 40.9 %all-to-all-start.3 = ((bf16[32,24,1024]{2,1,0:T(8,128)(2,1)}), bf16[32,24,1024]{2,1,0:T(8,128)(2,1)S(1)}, u32[]{:S(2)}, u32[]{:S(2)}) async-start(bf16[32,24,1024]{2,1,0:T(8,128)(2,1)} %bitcast.34), calls=%async_computation.3 | async-start | bytes 3145728 | tf_op jit(solution)/shard_map/all_to_all | solution.py:49
  331.1 18.4 %all-to-all-start.5 = ((f32[32,16,128]{2,1,0:T(8,128)}), f32[32,16,128]{2,1,0:T(8,128)S(1)}, u32[]{:S(2)}, u32[]{:S(2)}) async-start(f32[32,16,128]{2,1,0:T(8,128)} %broadcast_in_dim.66), calls=%async_computation.5 | async-start | bytes 524288 | tf_op jit(solution)/shard_map/all_to_all | solution.py:18
